TPU v7x, 32 devices: a whole 2x2x4 slice. The times are simulated.
32 devices in a mesh: grp: 4 (over y, x), mem: 8 (over z, core).
Axes of the slice: x: 2, y: 2, z: 4, core: 2. Of those that a mesh axis runs over, the one named last changes fastest.
Arguments:
- weight: bfloat16 [2, 16384, 16384], P(None, None, ('grp', 'mem')), may hold values from -0.046875 to 0.046875
- activation: bfloat16 [2, 16384, 512], P(None, ('grp', 'mem')), may hold values from -6 to 6
- points: int32 [4], replicated, may hold values from 0 to 3, each once
Outputs:
- share: float32 [4, 16384, 512], P('grp', 'mem')
Inputs may be any that keep to these rules, and one draw needn't show every extreme that they name: A permutation of 0 to 3; group g evaluates at points[g] + 1.
All inputs are finite; a program needn't handle non-finite values.
Results may differ from a plain program's by a relative error of at most 0.0042.
Values may be sent and summed in bfloat16 or wider, within the bound.
A program may use at most 320 MiB of HBM per device.

v0:
```python
import jax
import jax.numpy as jnp
from jax import lax
from jax.sharding import PartitionSpec as P


def code_stack(raw_blocks, factors):
    total = factors[:, 0, None, None] * raw_blocks[0].astype(jnp.float32)[None]
    for block in range(1, raw_blocks.shape[0]):
        total = total + factors[:, block, None, None] * raw_blocks[block].astype(jnp.float32)[None]
    return total.astype(jnp.bfloat16)


def per_device(weight, activation, points):
    groups = lax.axis_size("grp")
    blocks = weight.shape[0]
    splits = activation.shape[0]
    anchors = (points + 1).astype(jnp.float32) / groups
    factors = anchors[:, None] ** jnp.arange(blocks, dtype=jnp.float32)[None, :]
    lifts_all = anchors[:, None] ** (jnp.arange(splits, dtype=jnp.float32) * blocks)[None, :]
    slab = lax.all_to_all(weight, "mem", split_axis=1, concat_axis=2, tiled=True)
    block_input = lax.all_gather(activation, "mem", axis=1, tiled=True)
    coded_weight = code_stack(slab, factors)
    coded_input = code_stack(block_input, lifts_all)
    return lax.psum_scatter(
        jnp.einsum("grk,gkc->grc", coded_weight, coded_input, preferred_element_type=jnp.float32),
        "grp",
        scatter_dimension=0,
        tiled=True,
    )


def solution(mesh):
    placed = (P(None, None, ("grp", "mem")), P(None, ("grp", "mem"), None), P())
    return jax.shard_map(
        per_device, mesh=mesh, in_specs=placed, out_specs=P("grp", "mem", None), check_vma=False
    )
```

profile of v0, /device:TPU:0, one launch (start us, length us, event | category | flops | bytes accessed | tf_op | source)
XLA Modules:
  0.0 1254.2 jit_solution(2382327408538441488)
XLA Ops:
  6.5 60.1 %copy.10 = bf16[2,16384,512]{2,0,1:T(2,128)(2,1)} copy(bf16[2,16384,512]{2,1,0:T(8,128)(2,1)} %param.3) | data formatting | bytes 67108864 | tf_op args[0]
  66.6 0.0 copy-start
  66.6 7.2 all-to-all-start
  73.9 0.0 all-gather.2.cloned.1.call-start
  73.9 0.7 all-gather.2.cloned.1.call-update
  74.6 0.0 reduce-scatter.4.cloned.1.call-start
  74.7 0.0 copy-done
  74.7 0.1 broadcast_power_fusion
  74.8 154.4 %all-gather.2.cloned.1.call-done = bf16[2,4096,512]{2,1,0:T(8,128)(2,1)} async-done(((bf16[2,512,512]{2,1,0:T(8,128)(2,1)}), bf16[2,4096,512]{2,1,0:T(8,128)(2,1)}) %all-gather.2.cloned.1.call-update) | async-done | bytes 8388624 | tf_op jit(solution)/shard_map/all_gather | solution.py:22
  229.1 11.7 fusion.10
  240.9 15.1 %add_convert_fusion.10 = bf16[4,4096,512]{2,1,0:T(8,128)(2,1)} fusion(f32[4096,512]{1,0:T(8,128)} %get-tuple-element.8, f32[4]{0:T(128)S(1)} %get-tuple-element.10, f32[4096,512]{1,0:T(8,128)} %get-tuple-element.7, f32[4]{0:T(128)S(1)} %get-tuple-element.9), kind=kLoop, calls=%fused_computation.6.clone.clone.2 | loop fusion | flops 33554432 | bytes 33554464 | tf_op jit(solution)/shard_map/grk,gkc->grc/dot_general | solution.py:26
  256.0 609.3 %all-to-all-done = bf16[2,16384,512]{2,0,1:T(2,128)(2,1)} async-done(((bf16[2,16384,512]{2,0,1:T(2,128)(2,1)}), bf16[2,16384,512]{2,0,1:T(2,128)(2,1)}, u32[]{:S(2)}, u32[]{:S(2)}) %all-to-all-start) | async-done | bytes 33554464 | tf_op jit(solution)/shard_map/all_to_all | solution.py:21
  865.3 22.7 %copy.11 = bf16[2,16384,512]{2,1,0:T(8,128)(2,1)} copy(bf16[2,16384,512]{2,0,1:T(2,128)(2,1)} %all-to-all-done) | data formatting | bytes 67108864 | tf_op jit(solution)/shard_map/all_to_all | solution.py:21
  888.0 34.1 %slice_convert_fusion.1 = (f32[1,2048,8,512]{3,1,2,0:T(8,128)}, f32[1,2048,8,512]{3,1,2,0:T(8,128)}) fusion(bf16[2,2048,8,512]{3,1,2,0:T(8,128)(2,1)} %bitcast.25), kind=kLoop, calls=%fused_computation.8 | loop fusion | flops 16777216 | bytes 100663296 | tf_op jit(solution)/shard_map/convert_element_type | solution.py:8
  922.1 31.8 %copy.14 = f32[1,2048,8,512]{1,3,2,0:T(8,128)} copy(f32[1,2048,8,512]{3,1,2,0:T(8,128)} %get-tuple-element.6) | data formatting | bytes 67108864 | tf_op jit(solution)/shard_map/convert_element_type | solution.py:10
  953.9 31.1 %copy.15 = f32[2048,4096]{1,0:T(8,128)} copy(f32[2048,4096]{0,1:T(8,128)} %bitcast.26) | data formatting | bytes 67108864 | tf_op jit(solution)/shard_map/convert_element_type | solution.py:10
  985.0 31.8 %copy.12 = f32[1,2048,8,512]{1,3,2,0:T(8,128)} copy(f32[1,2048,8,512]{3,1,2,0:T(8,128)} %get-tuple-element.5) | data formatting | bytes 67108864 | tf_op jit(solution)/shard_map/convert_element_type | solution.py:8
  1016.8 31.1 %copy.13 = f32[2048,4096]{1,0:T(8,128)} copy(f32[2048,4096]{0,1:T(8,128)} %bitcast.27) | data formatting | bytes 67108864 | tf_op jit(solution)/shard_map/convert_element_type | solution.py:8
  1047.9 46.0 %fusion = f32[4,2048,512]{2,1,0:T(8,128)} fusion(f32[2048,4096]{1,0:T(8,128)} %copy.15, f32[4]{0:T(128)S(1)} %get-tuple-element.15, f32[2048,4096]{1,0:T(8,128)} %copy.13, f32[4]{0:T(128)S(1)} %get-tuple-element.16, bf16[4,4096,512]{2,1,0:T(8,128)(2,1)} %add_convert_fusion.10), kind=kOutput, calls=%fused_computation.1 | convolution fusion | flops 34493956096 | bytes 100663328 | tf_op jit(solution)/shard_map/grk,gkc->grc/dot_general | solution.py:26
  1093.9 0.0 reduce-scatter.4.cloned.1.call-update
  1094.0 153.4 %reduce-scatter.4.cloned.1.call-done = f32[1,2048,512]{2,1,0:T(8,128)} async-done(((f32[4,2048,512]{2,1,0:T(8,128)}), f32[1,2048,512]{2,1,0:T(8,128)}) %reduce-scatter.4.cloned.1.call-update) | async-done | bytes 4194320
  (3 shorter events, 0.0 us)
Async XLA Ops:
  66.6 8.0 copy-start
  66.6 798.7 %all-to-all-start = ((bf16[2,16384,512]{2,0,1:T(2,128)(2,1)}), bf16[2,16384,512]{2,0,1:T(2,128)(2,1)}, u32[]{:S(2)}, u32[]{:S(2)}) async-start(bf16[2,16384,512]{2,0,1:T(2,128)(2,1)} %copy.10), calls=%async_computation | async-start | bytes 67108864 | tf_op jit(solution)/shard_map/all_to_all | solution.py:21
  73.9 155.3 %all-gather.2.cloned.1.call-start = ((), (), s32[]{:S(2)}) async-start(), calls=%async_computation.2 | async-start | bytes 9437184 | tf_op jit(solution)/shard_map/all_gather | solution.py:22
  74.6 1172.8 %reduce-scatter.4.cloned.1.call-start = ((), (), s32[]{:S(2)}) async-start(), calls=%async_computation.3 | async-start | bytes 20971520
Sparse Core Ops, SparseCore 0:
  76.3 152.8 all-gather.1
  1094.1 153.2 reduce-scatter.3
where the time goes:
time: 1260 us; the launch traced here: 1250 us
  waiting for transfers between devices  918 us (73%)
  local copies, waits for them, and re-layouts  209 us (17%)
  other arithmetic  60.9 us (5%)
  matrix products  46 us (4%)
  between operations  13.5 us (1%)
    all_to_all x1, waiting for transfers between devices, per_device(): lax.all_to_all(weight, 'mem', split_axis=1, concat_axis=2, tiled=True)  609 us
    all_gather x1, waiting for transfers between devices, per_device(): block_input = lax.all_gather(activation, 'mem', axis=1, tiled=True)  154 us
    unnamed x3, waiting for transfers between devices  154 us
    convert_element_type x2, local copies, waits for them, and re-layouts, code_stack(): raw_blocks[block].astype(jnp.float32)[None]  62.9 us
    convert_element_type x2, local copies, waits for them, and re-layouts, code_stack(): total = factors[:, 0, None, None] * raw_blocks[0].astype(jnp.float32)[None]  62.9 us
    unnamed x3, local copies, waits for them, and re-layouts  60.1 us
    dot_general x1, matrix products, per_device(): jnp.einsum('grk,gkc->grc', coded_weight, coded_input, preferred_element_t...  46 us
    convert_element_type x1, other arithmetic, code_stack(): total = factors[:, 0, None, None] * raw_blocks[0].astype(jnp.float32)[None]  34.1 us
  transfers between devices with their start and end apart: 3, of which 3 were waited for; matrix products, arithmetic and copies ran while one was open for 2% of the time, Pallas kernels for 0%

commit v1 on v0

v1 whole, which is shorter than its diff:
```python
import jax
import jax.numpy as jnp
from jax import lax
from jax.experimental import pallas as pl
from jax.experimental.pallas import tpu as pltpu
from jax.sharding import PartitionSpec as P

PAIRS = 4
F32, BF16 = jnp.float32, jnp.bfloat16
MESH = pl.DeviceIdType.MESH


def loop(n, body):
    def step(i, carry):
        body(i)
        return carry

    lax.fori_loop(0, n, step, 0)


def make_kernel(groups, members, blocks, splits, rows, depth, cols, ra, rb):
    bits = groups.bit_length() - 1
    ring = members // 2
    half = groups // 2
    off = [groups - (groups >> s) for s in range(bits + 1)]

    def kernel(points, weight, act, out, wxa, wxb, xp, xs, wt, cw, asend, az, ag, bsend, bg, bz,
               x_s, x_r, w_s, wa_r, wb_r, ld, send, az_r, ag_r, bg_r, bz_r):
        me_g = lax.axis_index("grp")
        me_m = lax.axis_index("mem")
        z, core = me_m // 2, me_m % 2
        twin = (me_g, z * 2 + 1 - core)

        def along(sgn):
            return (me_g, ((z + sgn + ring) % ring) * 2 + core)

        def blend(o, v0, v1):
            return v0 + o * (v1 - v0)

        def bit_of(w):
            return (me_g // w) % 2

        def across(o, s):
            w0, w1 = 1 << (bits - 1 - s), 1 << s
            p0 = me_g + w0 - 2 * w0 * bit_of(w0)
            p1 = me_g + w1 - 2 * w1 * bit_of(w1)
            return (blend(o, p0, p1), me_m)

        def group_at(o, s, h, j):
            w0, w1 = 1 << (bits - 1 - s), 1 << s
            b0, b1 = bit_of(w0), bit_of(w1)
            b0, b1 = b0 + h - 2 * b0 * h, b1 + h - 2 * b1 * h
            g0 = (me_g // (2 * w0)) * (2 * w0) + b0 * w0 + j
            g1 = me_g % w1 + b1 * w1 + j * (2 * w1)
            return blend(o, g0, g1)

        def slot_at(o, s, h, j):
            w0, w1 = 1 << (bits - 1 - s), 1 << s
            b0, b1 = bit_of(w0), bit_of(w1)
            b0, b1 = b0 + h - 2 * b0 * h, b1 + h - 2 * b1 * h
            return blend(o, b0 * w0 + j, b1 + 2 * j)

        def remote(src, dst, ssem, rsem, dev):
            return pltpu.make_async_remote_copy(
                src_ref=src, dst_ref=dst, send_sem=ssem, recv_sem=rsem, device_id=dev, device_id_type=MESH)

        def arrived(ref, sem):
            pltpu.make_async_copy(ref, ref, sem).wait()

        def anchor(g):
            return (points[g] + 1).astype(F32) / groups

        def power(a, n):
            r = a
            for _ in range(n - 1):
                r = r * a
            return r

        barrier = pltpu.get_barrier_semaphore()
        peers = [twin, along(1), along(-1)] + [across(0, s) for s in range(bits)]
        for dev in peers:
            pl.semaphore_signal(barrier, inc=1, device_id=dev, device_id_type=MESH)
        pl.semaphore_wait(barrier, len(peers))

        def a_sign(c):
            return 1 - 2 * c

        def b_sign(c):
            return 1 - 2 * ((c % 2 + c // 2) % 2)

        def dest(sgn, t):
            return (z - sgn * (1 + t) + 2 * ring) % ring

        def base(is_a, c, zd, core_):
            lead = c * ra if is_a else 2 * ra + c * rb
            return pl.multiple_of((zd * 2 + core_) * rows + lead, 16)

        x_copy = remote(act, xp, x_s, x_r, twin)
        x_copy.start()

        def push_a(t):
            def body(c):
                zd = dest(a_sign(c), t)
                remote(weight.at[:, pl.ds(base(True, c, zd, 1 - core), ra), :], wxa.at[c, t],
                       w_s.at[0], wa_r.at[c, t], twin).start()
            loop(2, body)

        def push_b(c):
            def body(t):
                zd = dest(b_sign(c), t)
                remote(weight.at[:, pl.ds(base(False, c, zd, 1 - core), rb), :], wxb.at[c, t],
                       w_s.at[1], wb_r.at[c], twin).start()
            loop(ring, body)

        push_a(0)
        push_b(0)
        push_b(1)
        if ring > 2:
            push_a(1)
        loop(2 * PAIRS - 2, lambda c: push_b(c + 2))
        for t in range(2, ring):
            push_a(t)

        x_copy.wait_recv()
        step = min(32, depth)

        def code_input(g):
            lift = power(anchor(g), blocks)
            for h, src in enumerate((act, xp)):
                def body(r):
                    at = pl.ds(pl.multiple_of(r * step, step), step)
                    total = src[0, at, :].astype(F32)
                    for k in range(1, splits):
                        total = total + power(lift, k) * src[k, at, :].astype(F32)
                    xs[g, pl.ds(pl.multiple_of(h * depth + r * step, step), step), :] = total.astype(BF16)
                loop(depth // step, body)
        loop(groups, code_input)

        def tile_copies(is_a, c, t, sgn, slot):
            n = ra if is_a else rb
            wx = wxa if is_a else wxb
            own = pltpu.make_async_copy(
                weight.at[:, pl.ds(base(is_a, c, dest(sgn, t), core), n), :],
                wt.at[slot, 0, :, pl.ds(0, n), :], ld.at[slot, 0])
            other = pltpu.make_async_copy(wx.at[c, t], wt.at[slot, 1, :, pl.ds(0, n), :], ld.at[slot, 1])
            return own, other

        def product(slot, n, g):
            a = anchor(g)
            factors = [power(a, j) for j in range(1, blocks)]

            def body(r):
                at = pl.ds(pl.multiple_of(r * 16, 16), 16)
                for h in range(2):
                    total = wt[slot, h, 0, at, :].astype(F32)
                    for j in range(1, blocks):
                        total = total + factors[j - 1] * wt[slot, h, j, at, :].astype(F32)
                    cw[at, h * depth:(h + 1) * depth] = total.astype(BF16)
            loop(n // 16, body)
            return jnp.dot(cw[0:n, :], xs[g], preferred_element_type=F32)

        def a_hop(t):
            def body(c, slot):
                def per_group(g):
                    acc = product(slot, ra, g)
                    if t == 0:
                        src = asend.at[c, g]
                        asend[c, g] = acc.astype(BF16)
                    else:
                        src = az.at[c, t - 1, g]
                        arrived(src, az_r.at[c, t - 1, g])
                        az[c, t - 1, g] = (acc + az[c, t - 1, g].astype(F32)).astype(BF16)
                    remote(src, az.at[c, t, g], send.at[0 if t == 0 else 1], az_r.at[c, t, g],
                           along(a_sign(c))).start()
                loop(groups, per_group)
            return body

        def a_turn(c, slot):
            def per_group(i):
                h, j = 1 - i // half, i % half
                g = group_at(c, 0, h, j)
                acc = product(slot, ra, g)
                arrived(az.at[c, ring - 2, g], az_r.at[c, ring - 2, g])
                az[c, ring - 2, g] = (acc + az[c, ring - 2, g].astype(F32)).astype(BF16)

                @pl.when(i < half)
                def _():
                    remote(az.at[c, ring - 2, g], ag.at[c, j], send.at[2], ag_r.at[c, 0], across(c, 0)).start()
            loop(groups, per_group)

        def a_stage(s):
            def body(c):
                n = half >> (s - 1)
                arrived(ag.at[c, pl.ds(off[s - 1], n)], ag_r.at[c, s - 1])

                def held(j):
                    if s == 1:
                        return az[c, ring - 2, group_at(c, 0, 0, j)]
                    return ag[c, off[s - 2] + slot_at(c, s - 1, 0, j)]

                def summed(j):
                    return ag[c, off[s - 1] + j].astype(F32) + held(j).astype(F32)

                if s == bits:
                    out[0, pl.ds(pl.multiple_of(c * ra, 16), ra), :] = summed(0)
                    return

                def per_slot(i):
                    h, jj = 1 - i // (n // 2), i % (n // 2)
                    j = slot_at(c, s, h, jj)
                    ag[c, off[s - 1] + j] = summed(j).astype(BF16)

                    @pl.when(i < n // 2)
                    def _():
                        remote(ag.at[c, off[s - 1] + j], ag.at[c, off[s] + jj], send.at[3],
                               ag_r.at[c, s], across(c, s)).start()
                loop(n, per_slot)
            return body

        def b_first(c, t, slot):
            o = c % 2

            def per_slot(j):
                acc = product(slot, rb, group_at(o, 0, 1, j))
                bsend[c, t, j] = acc.astype(BF16)
                remote(bsend.at[c, t, j], bg.at[c, t, j], send.at[4], bg_r.at[c, t, 0], across(o, 0)).start()
            loop(half, per_slot)

        def b_merge(c, t, s, add):
            o = c % 2
            n = half >> (s - 1)
            arrived(bg.at[c, t, pl.ds(off[s - 1], n)], bg_r.at[c, t, s - 1])

            def per_slot(i):
                h, jj = 1 - i // (n // 2), i % (n // 2)
                j = slot_at(o, s, h, jj)
                bg[c, t, off[s - 1] + j] = (add(j) + bg[c, t, off[s - 1] + j].astype(F32)).astype(BF16)

                @pl.when(i < n // 2)
                def _():
                    remote(bg.at[c, t, off[s - 1] + j], bg.at[c, t, off[s] + jj], send.at[5],
                           bg_r.at[c, t, s], across(o, s)).start()
            loop(n, per_slot)

        def b_second(c, t, slot):
            b_merge(c, t, 1, lambda j: product(slot, rb, group_at(c % 2, 0, 0, j)))

        def b_middle(p, s):
            def body(i):
                c, t = 2 * p + i % 2, i // 2
                b_merge(c, t, s, lambda j: bg[c, t, off[s - 2] + slot_at(c % 2, s - 1, 0, j)].astype(F32))
            loop(2 * ring, body)

        def b_ring(p, t):
            def body(i):
                c = 2 * p + i
                last = off[bits - 1]
                arrived(bg.at[c, t, pl.ds(last, 1)], bg_r.at[c, t, bits - 1])
                kept = off[bits - 2] + slot_at(c % 2, bits - 1, 0, 0)
                val = bg[c, t, last].astype(F32) + bg[c, t, kept].astype(F32)
                if t > 0:
                    arrived(bz.at[c, t - 1], bz_r.at[c, t - 1])
                    val = val + bz[c, t - 1].astype(F32)
                if t == ring - 1:
                    out[0, pl.ds(pl.multiple_of(2 * ra + c * rb, 16), rb), :] = val
                    return
                if t == 0:
                    src = bg.at[c, t, last]
                    bg[c, t, last] = val.astype(BF16)
                else:
                    src = bz.at[c, t - 1]
                    bz[c, t - 1] = val.astype(BF16)
                remote(src, bz.at[c, t], send.at[6], bz_r.at[c, t], along(b_sign(c))).start()
            loop(2, body)

        def a_site(t, body):
            return ("tiles", True, True, 2, lambda i: (i, t), lambda c, t_, slot: body(c, slot))

        def b_site(p, first, body):
            return ("tiles", False, first, 2 * ring, lambda i: (2 * p + i % 2, i // 2), body)

        def plain(fn):
            return ("plain", fn)

        a_queue = [a_site(t, a_hop(t)) for t in range(1, ring - 1)] + [a_site(ring - 1, a_turn)]
        a_queue += [plain(lambda s=s: loop(2, a_stage(s))) for s in range(1, bits + 1)]
        queues, order = [], [a_site(0, a_hop(0))]

        def drain(with_a):
            for q in queues:
                if q:
                    order.append(q.pop(0))
            if with_a and a_queue:
                order.append(a_queue.pop(0))

        for p in range(PAIRS):
            order.append(b_site(p, True, b_first))
            drain(p == 1 or p > 2)
            order.append(b_site(p, False, b_second))
            drain(p > 0)
            queues.append([plain(lambda p=p, s=s: b_middle(p, s)) for s in range(2, bits)]
                          + [plain(lambda p=p, t=t: b_ring(p, t)) for t in range(ring)])
        while a_queue or any(queues):
            drain(True)

        def begin(site, i, slot):
            _, is_a, first, _, index, _ = site
            c, t = index(i)
            sgn = a_sign(c) if is_a else b_sign(c)
            own, other = tile_copies(is_a, c, t, sgn, slot)
            own.start()
            if is_a:
                arrived(wxa.at[c, t], wa_r.at[c, t])
            elif first:
                @pl.when(t == 0)
                def _():
                    arrived(wxb.at[c], wb_r.at[c])
            other.start()

        tiles = [s for s in order if s[0] == "tiles"]
        begin(tiles[0], 0, 0)
        at = 0
        for site in order:
            if site[0] == "plain":
                site[1]()
                continue
            at += 1
            follow = tiles[at] if at < len(tiles) else None
            _, is_a, first, count, index, body = site

            def run(i, site=site, follow=follow, is_a=is_a, count=count, index=index, body=body):
                slot = i % 2

                @pl.when(i + 1 < count)
                def _():
                    begin(site, i + 1, 1 - slot)

                if follow is not None:
                    @pl.when(i + 1 == count)
                    def _():
                        begin(follow, 0, 1 - slot)
                c, t = index(i)
                for cp in tile_copies(is_a, c, t, a_sign(c) if is_a else b_sign(c), slot):
                    cp.wait()
                body(c, t, slot)
            loop(count, run)

        x_copy.wait_send()
        arrived(wxa, w_s.at[0])
        arrived(wxb, w_s.at[1])
        arrived(asend, send.at[0])
        arrived(az.at[:, pl.ds(0, ring - 2)], send.at[1])
        arrived(ag.at[:, pl.ds(0, half)], send.at[2])
        arrived(ag.at[:, pl.ds(0, half - 1)], send.at[3])
        arrived(bsend, send.at[4])
        arrived(bg.at[:, :, pl.ds(0, half - 1)], send.at[5])
        arrived(bz, send.at[6])

    dma = pltpu.SemaphoreType.DMA
    nb = 2 * PAIRS
    shapes = [
        pltpu.VMEM((splits, depth, cols), BF16),
        pltpu.VMEM((groups, 2 * depth, cols), BF16),
        pltpu.VMEM((2, 2, blocks, max(ra, rb), depth), BF16),
        pltpu.VMEM((max(ra, rb), 2 * depth), BF16),
        pltpu.VMEM((2, groups, ra, cols), BF16),
        pltpu.VMEM((2, ring - 1, groups, ra, cols), BF16),
        pltpu.VMEM((2, groups - 1, ra, cols), BF16),
        pltpu.VMEM((nb, ring, half, rb, cols), BF16),
        pltpu.VMEM((nb, ring, groups - 1, rb, cols), BF16),
        pltpu.VMEM((nb, ring - 1, rb, cols), BF16),
        dma, dma, dma((2,)), dma((2, ring)), dma((nb,)), dma((2, 2)), dma((7,)),
        dma((2, ring - 1, groups)), dma((2, bits)), dma((nb, ring, bits)), dma((nb, ring - 1)),
    ]
    spaces = (pltpu.VMEM, pl.ANY, pl.ANY)
    return pl.pallas_call(
        kernel,
        name="coded_share",
        out_shape=(
            jax.ShapeDtypeStruct((1, rows, cols), F32),
            jax.ShapeDtypeStruct((2, ring, blocks, ra, depth), BF16),
            jax.ShapeDtypeStruct((nb, ring, blocks, rb, depth), BF16),
        ),
        in_specs=[
            pl.BlockSpec(memory_space=pltpu.SMEM),
            pl.BlockSpec(memory_space=pl.ANY),
            pl.BlockSpec(memory_space=pltpu.VMEM),
        ],
        out_specs=tuple(pl.BlockSpec(memory_space=m) for m in spaces),
        scratch_shapes=shapes,
        compiler_params=pltpu.CompilerParams(
            collective_id=0, has_side_effects=True, vmem_limit_bytes=67043328),
    )


def solution(mesh):
    groups, members = mesh.shape["grp"], mesh.shape["mem"]

    def per_device(weight, activation, points):
        blocks, height, depth = weight.shape
        splits, _, cols = activation.shape
        rows = height // members
        rb = (rows * 13 // 16) // (2 * PAIRS) // 16 * 16
        ra = (rows - 2 * PAIRS * rb) // 2
        call = make_kernel(groups, members, blocks, splits, rows, depth, cols, ra, rb)
        return call(points, weight, activation)[0]

    placed = (P(None, None, ("grp", "mem")), P(None, ("grp", "mem"), None), P())
    return jax.shard_map(
        per_device, mesh=mesh, in_specs=placed, out_specs=P("grp", "mem", None), check_vma=False)
```

time: 1260 us -> 288 us (0.23)
  waiting for transfers between devices: 918 us -> 0 us
  Pallas kernels: 0 us -> 284 us
  local copies, waits for them, and re-layouts: 209 us -> 4.64 us
  other arithmetic: 60.9 us -> 0 us
  matrix products: 46 us -> 0 us
  between operations: 13.5 us -> 0.01 us
    all_to_all x1 -> x0, waiting for transfers between devices: 609 us -> none  [per_device(): lax.all_to_all(weight, 'mem', split_axis=1, concat_axis=2, tiled=True)]
    pallas_call x0 -> x1, Pallas kernels: none -> 284 us  [per_device(): return call(points, weight, activation)[0]]
    all_gather x1 -> x0, waiting for transfers between devices: 154 us -> none  [per_device(): block_input = lax.all_gather(activation, 'mem', axis=1, tiled=True)]
    unnamed x3 -> x0, waiting for transfers between devices: 154 us -> none
    convert_element_type x4 -> x0, local copies, waits for them, and re-layouts: 126 us -> none  [the longest x2 62.9 us: code_stack(): raw_blocks[block].astype(jnp.float32)[None]]
    unnamed x3 -> x1, local copies, waits for them, and re-layouts: 60.1 us -> 4.64 us
    dot_general x1 -> x0, matrix products: 46 us -> none  [per_device(): jnp.einsum('grk,gkc->grc', coded_weight, coded_input, preferred_element_t...]
    convert_element_type x1 -> x0, other arithmetic: 34.1 us -> none  [code_stack(): total = factors[:, 0, None, None] * raw_blocks[0].astype(jnp.float32)[None]]
  transfers between devices with their start and end apart: 3 -> 0, of which waited for: 3 -> 0; matrix products, arithmetic and copies ran while one was open for 2% -> 0% of each run, Pallas kernels for 0% -> 0%
where the time goes in v1:
time: 288 us
  Pallas kernels  284 us (99%)
  local copies, waits for them, and re-layouts  4.64 us (2%)
    pallas_call x1, Pallas kernels, per_device(): return call(points, weight, activation)[0]  284 us

profile of v1, /device:TPU:0, one launch (start us, length us, event | category | flops | bytes accessed | tf_op | source)
XLA Modules:
  0.0 288.2 jit_solution(17748923309620303682)
XLA Ops:
  0.0 283.5 %coded_share.1 = (f32[1,2048,512]{2,1,0:T(8,128)}, bf16[2,4,2,192,512]{4,3,2,1,0:T(8,128)(2,1)}, bf16[8,4,2,208,512]{4,3,2,1,0:T(8,128)(2,1)}) custom-call(s32[4]{0:T(128)} %points.1, bf16[2,16384,512]{2,1,0:T(8,128)(2,1)} %weight.1, bf16[2,512,512]{2,1,0:T(8,128)(2,1)} %act.1), custom_call_target="tpu_custom_call" | custom-call | tf_op jit(solution)/shard_map/coded_share/pallas_call | solution.py:406
  283.5 4.6 %copy.5 = f32[1,2048,512]{2,1,0:T(8,128)} copy(f32[1,2048,512]{2,1,0:T(8,128)} %get-tuple-element.6) | data formatting | bytes 8388608

commit v2 on v1

--- a/solution.py
+++ b/solution.py
@@ -112,29 +112,33 @@
                        w_s.at[1], wb_r.at[c], twin).start()
             loop(ring, body)
 
-        push_a(0)
         push_b(0)
         push_b(1)
+        push_a(0)
         if ring > 2:
             push_a(1)
         loop(2 * PAIRS - 2, lambda c: push_b(c + 2))
         for t in range(2, ring):
             push_a(t)
 
+        step = min(16, depth)
+        lifts = [power(anchor(g), blocks) for g in range(groups)]
+
+        def code_input(h, src):
+            def body(r):
+                at = pl.ds(pl.multiple_of(r * step, step), step)
+                to = pl.ds(pl.multiple_of(h * depth + r * step, step), step)
+                parts = [src[k, at, :].astype(F32) for k in range(splits)]
+                for g in range(groups):
+                    total = parts[0]
+                    for k in range(1, splits):
+                        total = total + power(lifts[g], k) * parts[k]
+                    xs[g, to, :] = total.astype(BF16)
+            loop(depth // step, body)
+
+        code_input(0, act)
         x_copy.wait_recv()
-        step = min(32, depth)
-
-        def code_input(g):
-            lift = power(anchor(g), blocks)
-            for h, src in enumerate((act, xp)):
-                def body(r):
-                    at = pl.ds(pl.multiple_of(r * step, step), step)
-                    total = src[0, at, :].astype(F32)
-                    for k in range(1, splits):
-                        total = total + power(lift, k) * src[k, at, :].astype(F32)
-                    xs[g, pl.ds(pl.multiple_of(h * depth + r * step, step), step), :] = total.astype(BF16)
-                loop(depth // step, body)
-        loop(groups, code_input)
+        code_input(1, xp)
 
         def tile_copies(is_a, c, t, sgn, slot):
             n = ra if is_a else rb
@@ -150,13 +154,14 @@
             factors = [power(a, j) for j in range(1, blocks)]
 
             def body(r):
-                at = pl.ds(pl.multiple_of(r * 16, 16), 16)
+                at = pl.ds(r * 16, 16)
                 for h in range(2):
                     total = wt[slot, h, 0, at, :].astype(F32)
                     for j in range(1, blocks):
                         total = total + factors[j - 1] * wt[slot, h, j, at, :].astype(F32)
                     cw[at, h * depth:(h + 1) * depth] = total.astype(BF16)
-            loop(n // 16, body)
+            for r in range(n // 16):
+                body(r)
             return jnp.dot(cw[0:n, :], xs[g], preferred_element_type=F32)
 
         def a_hop(t):
@@ -282,26 +287,34 @@
         def plain(fn):
             return ("plain", fn)
 
+        def b_tail(p):
+            middle = [plain(lambda s=s: b_middle(p, s)) for s in range(2, bits)]
+            return middle + [plain(lambda t=t: b_ring(p, t)) for t in range(ring)]
+
         a_queue = [a_site(t, a_hop(t)) for t in range(1, ring - 1)] + [a_site(ring - 1, a_turn)]
         a_queue += [plain(lambda s=s: loop(2, a_stage(s))) for s in range(1, bits + 1)]
-        queues, order = [], [a_site(0, a_hop(0))]
-
-        def drain(with_a):
+        queues, order = [], [b_site(0, True, b_first), a_site(0, a_hop(0))]
+
+        def drain():
             for q in queues:
                 if q:
                     order.append(q.pop(0))
-            if with_a and a_queue:
+
+        for p in range(PAIRS):
+            order.append(b_site(p, False, b_second))
+            if p + 1 == PAIRS:
+                break
+            order.append(b_site(p + 1, True, b_first))
+            queues.append(b_tail(p))
+            drain()
+            if len(a_queue) > bits + 1:
                 order.append(a_queue.pop(0))
-
-        for p in range(PAIRS):
-            order.append(b_site(p, True, b_first))
-            drain(p == 1 or p > 2)
-            order.append(b_site(p, False, b_second))
-            drain(p > 0)
-            queues.append([plain(lambda p=p, s=s: b_middle(p, s)) for s in range(2, bits)]
-                          + [plain(lambda p=p, t=t: b_ring(p, t)) for t in range(ring)])
+            drain()
+        queues.append(b_tail(PAIRS - 1))
         while a_queue or any(queues):
-            drain(True)
+            if a_queue:
+                order.append(a_queue.pop(0))
+            drain()
 
         def begin(site, i, slot):
             _, is_a, first, _, index, _ = site

time: 288 us -> 275 us (0.955)
  Pallas kernels: 284 us -> 269 us
    pallas_call x1, Pallas kernels: 284 us -> 269 us  [per_device(): return call(points, weight, activation)[0]]
where the time goes in v2:
time: 275 us; the launch traced here: 274 us
  Pallas kernels  269 us (98%)
  local copies, waits for them, and re-layouts  4.64 us (2%)
    pallas_call x1, Pallas kernels, per_device(): return call(points, weight, activation)[0]  269 us

profile of v2, /device:TPU:0, one launch (start us, length us, event | category | flops | bytes accessed | tf_op | source)
XLA Modules:
  0.0 273.9 jit_solution(4846884492180904871)
XLA Ops:
  0.0 269.3 %coded_share.1 = (f32[1,2048,512]{2,1,0:T(8,128)}, bf16[2,4,2,192,512]{4,3,2,1,0:T(8,128)(2,1)}, bf16[8,4,2,208,512]{4,3,2,1,0:T(8,128)(2,1)}) custom-call(s32[4]{0:T(128)} %points.1, bf16[2,16384,512]{2,1,0:T(8,128)(2,1)} %weight.1, bf16[2,512,512]{2,1,0:T(8,128)(2,1)} %act.1), custom_call_target="tpu_custom_call" | custom-call | tf_op jit(solution)/shard_map/coded_share/pallas_call | solution.py:419
  269.3 4.6 %copy.5 = f32[1,2048,512]{2,1,0:T(8,128)} copy(f32[1,2048,512]{2,1,0:T(8,128)} %get-tuple-element.6) | data formatting | bytes 8388608
